TPU v7x, 32 devices: a whole 2x2x4 slice. The times are simulated.
32 devices in a mesh: groups: 2 (over x), blk: 16 (over z, y, core).
Axes of the slice: x: 2, y: 2, z: 4, core: 2. Of those that a mesh axis runs over, the one named last changes fastest.
Arguments:
- embeddings: bfloat16 [12288, 512], P(('groups', 'blk')), parts along dimension 0, may hold values from -24 to 24
- cluster_ids: int32 [12288], P(('groups', 'blk')), parts along dimension 0, may hold values from 0 to 63, as said below
- cluster_sizes: int32 [128], P('groups'), parts along dimension 0, may hold values from 12 to 960, as said below
Outputs:
- log_density: float32 [12288], P(('groups', 'blk')), parts along dimension 0
- centrality: float32 [12288], P(('groups', 'blk')), parts along dimension 0
There are 2 independent parts, one for each index of `groups`. A program takes and returns all parts, laid end to end along the dimension named above; each array names one. Nothing has to cross between parts.
Inputs may be any that keep to these rules, and one draw needn't show every extreme that they name: cluster_sizes[c] is the number of rows whose cluster id is c; the sizes sum to 6144 and the largest is exactly 960. `cluster_ids`: rows are dealt to the devices of blk: with n the number of devices of blk and E_c the sum of cluster_sizes[c'] mod n over the clusters c' < c, device s holds cluster_sizes[c] // n rows of cluster c, plus one more exactly when (s - E_c) mod n < cluster_sizes[c] mod n. Within a device the rows stand in no particular order.
All inputs are finite; a program needn't handle non-finite values.
Results may differ from a plain program's by a relative error of at most 0.00065.
The roundings to bfloat16 on the way count: a program that leaves them out, or rounds other values in their place, can miss the bound.
Values may be sent and summed in bfloat16 or wider, within the bound.
No kernel may reach another device: no remote copies, remote signals or barrier semaphores. Data moves between devices by JAX's collectives and lax.ppermute only.
A program may use at most 64 MiB of HBM per device.

v0:
```python
import jax
import jax.numpy as jnp
from jax import lax
from jax.sharding import PartitionSpec as P

SOFTMAX_TEMP = 0.1
EPSILON = 1e-06


def shifted(array, axis, by):
    peers = lax.axis_size(axis)
    pairs = [(i, i + by) for i in range(peers) if 0 <= i + by < peers]
    return lax.ppermute(array, axis, pairs)


def unit_rows(embeddings):
    values = embeddings.astype(jnp.float32)
    scale = lax.rsqrt(jnp.mean(values * values, axis=1, keepdims=True) + EPSILON)
    return (values * (scale * values.shape[1] ** (-0.5))).astype(jnp.bfloat16)


def block_terms(remaining_rows, left_labels, right_rows, right_labels):
    similarity_scores = jnp.einsum(
        "rd,kd->rk", remaining_rows, right_rows, preferred_element_type=jnp.float32
    )
    same_cluster = left_labels[:, None] == right_labels[None, :]
    return jnp.sum(jnp.where(same_cluster, jnp.exp(similarity_scores / SOFTMAX_TEMP), 0.0), axis=1)


def lookup(table, one_hot):
    return jnp.sum(jnp.where(one_hot, table[None, :], 0), axis=1)


def sorted_density(unit, cluster_sizes, member):
    devices = lax.axis_size("blk")
    own_index = lax.axis_index("blk")
    rows_dev = unit.shape[0]
    clusters = cluster_sizes.shape[0]
    total_rows = rows_dev * devices
    fewest = total_rows // 512
    largest = total_rows * 5 // 32
    capacity = min(rows_dev, rows_dev // devices + rows_dev // fewest + 2)
    reach = (largest + rows_dev - 2) // rows_dev
    ends = jnp.cumsum(cluster_sizes)
    starts = ends - cluster_sizes
    base = cluster_sizes // devices
    extra = cluster_sizes % devices
    first = (jnp.cumsum(extra) - extra) % devices
    source_rows = jnp.arange(devices, dtype=jnp.int32)
    holds = base[None, :] + (
        (source_rows[:, None] - first[None, :]) % devices < extra[None, :]
    ).astype(jnp.int32)
    member_count = jnp.cumsum(member.astype(jnp.int32), axis=0)
    rank = jnp.sum(jnp.where(member, member_count - 1, 0), axis=1)
    held_row = jnp.dot(
        member.astype(jnp.float32), holds.T.astype(jnp.float32), precision=lax.Precision.HIGHEST
    ).astype(jnp.int32)
    before_me = (source_rows[None, :] < own_index) & (held_row > rank[:, None])
    within = jnp.sum(jnp.minimum(held_row, rank[:, None]), axis=1) + jnp.sum(
        before_me.astype(jnp.int32), axis=1
    )
    position = lookup(starts, member) + within
    target = position // rows_dev
    earlier = (target[None, :] == target[:, None]) & (position[None, :] < position[:, None])
    slot = jnp.sum(earlier.astype(jnp.int32), axis=1)
    address = target * capacity + slot
    sender = (
        jnp.zeros((devices * capacity,), jnp.int32)
        .at[address]
        .set(jnp.arange(rows_dev, dtype=jnp.int32))
    )
    filled = jnp.zeros((devices * capacity,), jnp.bool_).at[address].set(True)
    packed = jnp.where(filled[:, None], unit[sender], jnp.zeros((), jnp.bfloat16))
    arrived = lax.all_to_all(packed, "blk", split_axis=0, concat_axis=0, tiled=True)
    local = jnp.arange(rows_dev, dtype=jnp.int32)
    places = own_index * rows_dev + local
    home_label = jnp.sum((places[:, None] >= ends[None, :]).astype(jnp.int32), axis=1)
    home_cluster_member = home_label[:, None] == jnp.arange(clusters, dtype=jnp.int32)[None, :]
    offset_in = places - lookup(starts, home_cluster_member)
    base_row = lookup(base, home_cluster_member)
    extra_row = lookup(extra, home_cluster_member)
    first_row = lookup(first, home_cluster_member)
    full_rounds = devices * base_row
    surplus = offset_in - full_rounds
    wrapped = first_row + extra_row - devices
    late_source = jnp.where(
        wrapped > 0,
        jnp.where(surplus < wrapped, surplus, first_row + surplus - wrapped),
        first_row + surplus,
    )
    anchor = jnp.where(offset_in < full_rounds, offset_in % devices, late_source)
    anchor_hot = anchor[:, None] == source_rows[None, :]
    anchor_count = jnp.cumsum(anchor_hot.astype(jnp.int32), axis=0)
    order_in = jnp.sum(jnp.where(anchor_hot, anchor_count - 1, 0), axis=1)
    block = arrived[anchor * capacity + order_in]

    def labels_at(spots):
        inside = (spots >= 0) & (spots < total_rows)
        found = jnp.sum((spots[:, None] >= ends[None, :]).astype(jnp.int32), axis=1)
        return jnp.where(inside, found, -1)

    density = block_terms(block, home_label, block, home_label)

    def advance(offset, carried_rows):
        upper, lower, running = carried_rows
        upper = shifted(upper, "blk", 1)
        lower = shifted(lower, "blk", -1)
        running = running + block_terms(
            block, home_label, upper, labels_at(places - offset * rows_dev)
        )
        running = running + block_terms(
            block, home_label, lower, labels_at(places + offset * rows_dev)
        )
        return (upper, lower, running)

    carried_out = lax.fori_loop(1, reach + 1, advance, (block, block, density))
    density = carried_out[2]
    returned = (
        jnp.zeros((devices * capacity,), jnp.float32).at[anchor * capacity + order_in].set(density)
    )
    answered = lax.all_to_all(returned, "blk", split_axis=0, concat_axis=0, tiled=True)
    return answered[address]


def on_device(embeddings, cluster_ids, cluster_sizes):
    unit = unit_rows(embeddings)
    clusters = cluster_sizes.shape[0]
    member = cluster_ids[:, None] == jnp.arange(clusters, dtype=jnp.int32)[None, :]
    partial_sum = jnp.einsum(
        "rc,rd->cd", member.astype(jnp.bfloat16), unit, preferred_element_type=jnp.float32
    )
    centroid = lax.psum(partial_sum, "blk")
    density = sorted_density(unit, cluster_sizes, member)
    sizes_row = lookup(cluster_sizes, member).astype(jnp.float32)
    log_density = jnp.log(density / sizes_row)
    projected = jnp.dot(unit.astype(jnp.float32), centroid.T, precision=lax.Precision.HIGHEST)
    centrality = jnp.sum(jnp.where(member, projected, 0.0), axis=1) / sizes_row
    return (log_density, centrality)


def solution(mesh):
    in_specs = (P(("groups", "blk"), None), P(("groups", "blk")), P("groups"))
    out_specs = (P(("groups", "blk")), P(("groups", "blk")))
    return jax.shard_map(
        on_device, mesh=mesh, in_specs=in_specs, out_specs=out_specs, check_vma=False
    )
```

profile of v0, /device:TPU:8, one launch (start us, length us, event | category | flops | bytes accessed | tf_op | source)
XLA Modules:
  0.0 142.4 jit_solution(12733876175211087510)
XLA Ops:
  7.2 1.2 fusion.14
  8.4 0.1 fusion.15
  8.6 0.0 copy-start.2
  8.6 0.6 copy-done.2
  9.2 0.1 copy.17
  9.3 0.1 reduce-window.37
  9.4 0.1 reduce
  9.5 0.1 copy.18
  9.6 0.1 reduce-window.38
  9.7 0.1 reduce.1
  9.9 0.0 copy-start.1
  9.9 0.1 convert_reduce_fusion.3
  10.0 0.6 copy-done.1
  10.6 0.9 reduce-window.41
  11.5 0.2 slice_reduce_fusion
  11.7 0.2 select_reduce_fusion
  11.9 0.3 convert_reduce_fusion.4
  12.3 0.3 convert_reduce_fusion.2
  12.6 2.9 %scatter_custom_fusion.1 = s32[928]{0:T(1024)S(1)} fusion(s32[384]{0:T(512)S(1)} %fusion.58, s32[384]{0:T(512)S(1)} %iota.57, s32[]{:T(128)} %copy.40), kind=kCustom, calls=%fused_computation.120 | custom fusion | bytes 3716 | tf_op jit(solution)/shard_map/scatter | solution.py:70
  15.5 4.0 %gather_fusion = bf16[928,512]{1,0:T(8,128)(2,1)S(1)} fusion(bf16[384,512]{1,0:T(8,128)(2,1)S(1)} %fusion.15, s32[1024]{0:T(1024)S(1)} %pad_clamp_fusion.2), kind=kCustom, calls=%fused_computation | custom fusion | bytes 1904256 | tf_op jit(solution)/shard_map/gather | solution.py:73
  19.6 0.2 gather.12
  19.8 2.0 %scatter_custom_fusion = pred[928]{0:T(1024)(128)(4,1)S(1)} fusion(s32[384]{0:T(512)S(1)} %fusion.58, pred[384]{0:T(512)(128)(4,1)S(1)} %broadcast.470, pred[]{:T(512)} %constant.152.clone.1), kind=kCustom, calls=%fused_computation.132 | custom fusion | bytes 929 | tf_op jit(solution)/shard_map/scatter | solution.py:72
  21.8 0.1 broadcast_in_dim.158
  21.9 1.2 broadcast_select_fusion
  23.1 6.3 %all-to-all-start = ((bf16[16,58,512]{2,1,0:T(8,128)(2,1)}), bf16[16,58,512]{2,1,0:T(8,128)(2,1)S(1)}, u32[]{:S(2)}, u32[]{:S(2)}) async-start(bf16[16,58,512]{2,1,0:T(8,128)(2,1)} %broadcast_select_fusion), calls=%async_computation | async-start | bytes 2097152 | tf_op jit(solution)/shard_map/all_to_all | solution.py:74
  29.4 0.0 all-reduce.2.cloned.1.call-start
  29.5 0.8 fusion.18
  30.3 0.0 all-reduce.2.cloned.1.call-update
  30.4 0.9 reduce-window.39
  31.2 0.2 slice_reduce_fusion.1
  31.5 0.1 fusion.34
  31.7 22.5 %all-to-all-done = bf16[16,58,512]{2,1,0:T(8,128)(2,1)S(1)} async-done(((bf16[16,58,512]{2,1,0:T(8,128)(2,1)}), bf16[16,58,512]{2,1,0:T(8,128)(2,1)S(1)}, u32[]{:S(2)}, u32[]{:S(2)}) %all-to-all-start) | async-done | bytes 950304 | tf_op jit(solution)/shard_map/all_to_all | solution.py:74
  54.2 0.3 all_to_all.15
  54.4 2.1 %gather_fusion.1 = bf16[384,512]{1,0:T(8,128)(2,1)S(1)} fusion(bf16[928,512]{1,0:T(8,128)(2,1)S(1)} %all_to_all.15, s32[1024]{0:T(1024)S(1)} %pad_clamp_fusion.1), kind=kCustom, calls=%fused_computation.1 | custom fusion | bytes 787968 | tf_op jit(solution)/shard_map/gather | solution.py:95
  56.6 0.4 fusion.12
  57.0 38.6 %while.18 = (s32[]{:T(128)}, bf16[384,512]{1,0:T(8,128)(2,1)S(1)}, bf16[384,512]{1,0:T(8,128)(2,1)S(1)}, f32[384]{0:T(512)S(1)}, s32[384]{0:T(512)S(1)}, /*index...) while((s32[]{:T(128)}, bf16[384,512]{1,0:T(8,128)(2,1)S(1)}, ...), condition=%wide.region_26.27_spmd.clone, body=%wide.region_21.26_spmd.clone.sunk | while | flops 303321984 | bytes 6322649 | solution.py:116
  57.0 2.9 %collective-permute-start = (bf16[384,512]{1,0:T(8,128)(2,1)S(1)}, bf16[384,512]{1,0:T(8,128)(2,1)S(1)}, u32[]{:S(2)}, u32[]{:S(2)}) collective-permute-start(bf16[384,512]{1,0:T(8,128)(2,1)S(1)} %get-tuple-element.275), channel_id=1, source_target_pairs={{0,1},{1,2},{2,3},{3,4},{4,5},{5,6},{6,7},{7,8},{8,9},{9,10},{10,1... | collective-permute-start | bytes 1179656 | tf_op jit(solution)/shard_map/while/body/eval_jaxpr/ppermute | solution.py:13
  59.9 3.5 %collective-permute-start.1 = (bf16[384,512]{1,0:T(8,128)(2,1)S(1)}, bf16[384,512]{1,0:T(8,128)(2,1)S(1)}, u32[]{:S(2)}, u32[]{:S(2)}) collective-permute-start(bf16[384,512]{1,0:T(8,128)(2,1)S(1)} %get-tuple-element.276), channel_id=1, source_target_pairs={{1,0},{2,1},{3,2},{4,3},{5,4},{6,5},{7,6},{8,7},{9,8},{10,9},{11,1... | collective-permute-start | bytes 1179656 | tf_op jit(solution)/shard_map/while/body/eval_jaxpr/ppermute | solution.py:13
  63.5 0.1 convert_reduce_fusion.6
  63.6 5.1 %collective-permute-done.1 = bf16[384,512]{1,0:T(8,128)(2,1)S(1)} collective-permute-done((bf16[384,512]{1,0:T(8,128)(2,1)S(1)}, bf16[384,512]{1,0:T(8,128)(2,1)S(1)}, u32[]{:S(2)}, u32[]{:S(2)}) %collective-permute-start.1) | collective-permute-done | bytes 393248 | tf_op jit(solution)/shard_map/while/body/eval_jaxpr/ppermute | solution.py:13
  68.7 0.4 fusion.89
  69.2 0.4 fusion.90
  69.7 4.3 %collective-permute-start = (bf16[384,512]{1,0:T(8,128)(2,1)S(1)}, bf16[384,512]{1,0:T(8,128)(2,1)S(1)}, u32[]{:S(2)}, u32[]{:S(2)}) collective-permute-start(bf16[384,512]{1,0:T(8,128)(2,1)S(1)} %get-tuple-element.275), channel_id=1, source_target_pairs={{0,1},{1,2},{2,3},{3,4},{4,5},{5,6},{6,7},{7,8},{8,9},{9,10},{10,1... | collective-permute-start | bytes 1179656 | tf_op jit(solution)/shard_map/while/body/eval_jaxpr/ppermute | solution.py:13
  74.0 2.3 %collective-permute-start.1 = (bf16[384,512]{1,0:T(8,128)(2,1)S(1)}, bf16[384,512]{1,0:T(8,128)(2,1)S(1)}, u32[]{:S(2)}, u32[]{:S(2)}) collective-permute-start(bf16[384,512]{1,0:T(8,128)(2,1)S(1)} %get-tuple-element.276), channel_id=1, source_target_pairs={{1,0},{2,1},{3,2},{4,3},{5,4},{6,5},{7,6},{8,7},{9,8},{10,9},{11,1... | collective-permute-start | bytes 1179656 | tf_op jit(solution)/shard_map/while/body/eval_jaxpr/ppermute | solution.py:13
  76.3 0.1 convert_reduce_fusion.6
  76.5 5.2 %collective-permute-done.1 = bf16[384,512]{1,0:T(8,128)(2,1)S(1)} collective-permute-done((bf16[384,512]{1,0:T(8,128)(2,1)S(1)}, bf16[384,512]{1,0:T(8,128)(2,1)S(1)}, u32[]{:S(2)}, u32[]{:S(2)}) %collective-permute-start.1) | collective-permute-done | bytes 393248 | tf_op jit(solution)/shard_map/while/body/eval_jaxpr/ppermute | solution.py:13
  81.7 0.4 fusion.89
  82.1 0.4 fusion.90
  82.6 4.2 %collective-permute-start = (bf16[384,512]{1,0:T(8,128)(2,1)S(1)}, bf16[384,512]{1,0:T(8,128)(2,1)S(1)}, u32[]{:S(2)}, u32[]{:S(2)}) collective-permute-start(bf16[384,512]{1,0:T(8,128)(2,1)S(1)} %get-tuple-element.275), channel_id=1, source_target_pairs={{0,1},{1,2},{2,3},{3,4},{4,5},{5,6},{6,7},{7,8},{8,9},{9,10},{10,1... | collective-permute-start | bytes 1179656 | tf_op jit(solution)/shard_map/while/body/eval_jaxpr/ppermute | solution.py:13
  86.8 2.4 %collective-permute-start.1 = (bf16[384,512]{1,0:T(8,128)(2,1)S(1)}, bf16[384,512]{1,0:T(8,128)(2,1)S(1)}, u32[]{:S(2)}, u32[]{:S(2)}) collective-permute-start(bf16[384,512]{1,0:T(8,128)(2,1)S(1)} %get-tuple-element.276), channel_id=1, source_target_pairs={{1,0},{2,1},{3,2},{4,3},{5,4},{6,5},{7,6},{8,7},{9,8},{10,9},{11,1... | collective-permute-start | bytes 1179656 | tf_op jit(solution)/shard_map/while/body/eval_jaxpr/ppermute | solution.py:13
  89.3 0.1 convert_reduce_fusion.6
  89.4 5.2 %collective-permute-done.1 = bf16[384,512]{1,0:T(8,128)(2,1)S(1)} collective-permute-done((bf16[384,512]{1,0:T(8,128)(2,1)S(1)}, bf16[384,512]{1,0:T(8,128)(2,1)S(1)}, u32[]{:S(2)}, u32[]{:S(2)}) %collective-permute-start.1) | collective-permute-done | bytes 393248 | tf_op jit(solution)/shard_map/while/body/eval_jaxpr/ppermute | solution.py:13
  94.6 0.4 fusion.89
  95.0 0.4 fusion.90
  95.5 2.9 %scatter_custom_fusion.2 = f32[928]{0:T(1024)S(1)} fusion(s32[384]{0:T(512)S(1)} %fusion.57, f32[384]{0:T(512)S(1)} %get-tuple-element.141, f32[]{:T(128)} %constant.139.clone.1), kind=kCustom, calls=%fused_computation.128 | custom fusion | bytes 3716 | tf_op jit(solution)/shard_map/scatter | solution.py:119
  98.5 0.7 all_to_all.16
  99.1 8.8 %all-to-all-start.1 = ((f32[16,58,1]{1,2,0:T(1,128)}), f32[16,58,1]{1,2,0:T(1,128)S(1)}, u32[]{:S(2)}, u32[]{:S(2)}) async-start(f32[16,58,1]{1,2,0:T(1,128)} %bitcast.9), calls=%async_computation.1 | async-start | bytes 16384 | tf_op jit(solution)/shard_map/all_to_all | solution.py:121
  107.9 22.5 %all-reduce.2.cloned.1.call-done = f32[64,512]{1,0:T(8,128)} async-done(((f32[64,512]{1,0:T(8,128)}), f32[64,512]{1,0:T(8,128)}) %all-reduce.2.cloned.1.call-update) | async-done | bytes 131088 | tf_op jit(solution)/shard_map/psum | solution.py:132
  130.4 1.4 fusion.13
  131.8 0.5 broadcast.549
  132.3 0.7 reduce.13
  133.0 0.1 all_to_all.18
  133.0 1.9 %gather_fusion.2 = f32[384]{0:T(512)S(1)} fusion(f32[928]{0:T(1024)S(1)} %all_to_all.18, s32[1024]{0:T(1024)S(1)} %pad_clamp_fusion), kind=kCustom, calls=%fused_computation.2 | custom fusion | bytes 4608 | tf_op jit(solution)/shard_map/gather | solution.py:122
  134.9 0.6 convert_divide_fusion
  (46 shorter events, 0.6 us)
Async XLA Ops:
  7.2 1.2 copy-start
  8.6 0.7 copy-start.2
  9.9 0.7 copy-start.1
  23.1 31.0 %all-to-all-start = ((bf16[16,58,512]{2,1,0:T(8,128)(2,1)}), bf16[16,58,512]{2,1,0:T(8,128)(2,1)S(1)}, u32[]{:S(2)}, u32[]{:S(2)}) async-start(bf16[16,58,512]{2,1,0:T(8,128)(2,1)} %broadcast_select_fusion), calls=%async_computation | async-start | bytes 2097152 | tf_op jit(solution)/shard_map/all_to_all | solution.py:74
  29.4 101.0 %all-reduce.2.cloned.1.call-start = ((), (), s32[]{:S(2)}) async-start(), calls=%async_computation.2 | async-start | bytes 262144 | tf_op jit(solution)/shard_map/psum | solution.py:132
  57.0 12.2 %collective-permute-start = (bf16[384,512]{1,0:T(8,128)(2,1)S(1)}, bf16[384,512]{1,0:T(8,128)(2,1)S(1)}, u32[]{:S(2)}, u32[]{:S(2)}) collective-permute-start(bf16[384,512]{1,0:T(8,128)(2,1)S(1)} %get-tuple-element.275), channel_id=1, source_target_pairs={{0,1},{1,2},{2,3},{3,4},{4,5},{5,6},{6,7},{7,8},{8,9},{9,10},{10,1... | collective-permute-start | bytes 1179656 | tf_op jit(solution)/shard_map/while/body/eval_jaxpr/ppermute | solution.py:13
  59.9 8.8 %collective-permute-start.1 = (bf16[384,512]{1,0:T(8,128)(2,1)S(1)}, bf16[384,512]{1,0:T(8,128)(2,1)S(1)}, u32[]{:S(2)}, u32[]{:S(2)}) collective-permute-start(bf16[384,512]{1,0:T(8,128)(2,1)S(1)} %get-tuple-element.276), channel_id=1, source_target_pairs={{1,0},{2,1},{3,2},{4,3},{5,4},{6,5},{7,6},{8,7},{9,8},{10,9},{11,1... | collective-permute-start | bytes 1179656 | tf_op jit(solution)/shard_map/while/body/eval_jaxpr/ppermute | solution.py:13
  69.7 12.4 %collective-permute-start = (bf16[384,512]{1,0:T(8,128)(2,1)S(1)}, bf16[384,512]{1,0:T(8,128)(2,1)S(1)}, u32[]{:S(2)}, u32[]{:S(2)}) collective-permute-start(bf16[384,512]{1,0:T(8,128)(2,1)S(1)} %get-tuple-element.275), channel_id=1, source_target_pairs={{0,1},{1,2},{2,3},{3,4},{4,5},{5,6},{6,7},{7,8},{8,9},{9,10},{10,1... | collective-permute-start | bytes 1179656 | tf_op jit(solution)/shard_map/while/body/eval_jaxpr/ppermute | solution.py:13
  74.0 7.7 %collective-permute-start.1 = (bf16[384,512]{1,0:T(8,128)(2,1)S(1)}, bf16[384,512]{1,0:T(8,128)(2,1)S(1)}, u32[]{:S(2)}, u32[]{:S(2)}) collective-permute-start(bf16[384,512]{1,0:T(8,128)(2,1)S(1)} %get-tuple-element.276), channel_id=1, source_target_pairs={{1,0},{2,1},{3,2},{4,3},{5,4},{6,5},{7,6},{8,7},{9,8},{10,9},{11,1... | collective-permute-start | bytes 1179656 | tf_op jit(solution)/shard_map/while/body/eval_jaxpr/ppermute | solution.py:13
  82.6 12.4 %collective-permute-start = (bf16[384,512]{1,0:T(8,128)(2,1)S(1)}, bf16[384,512]{1,0:T(8,128)(2,1)S(1)}, u32[]{:S(2)}, u32[]{:S(2)}) collective-permute-start(bf16[384,512]{1,0:T(8,128)(2,1)S(1)} %get-tuple-element.275), channel_id=1, source_target_pairs={{0,1},{1,2},{2,3},{3,4},{4,5},{5,6},{6,7},{7,8},{8,9},{9,10},{10,1... | collective-permute-start | bytes 1179656 | tf_op jit(solution)/shard_map/while/body/eval_jaxpr/ppermute | solution.py:13
  86.8 7.7 %collective-permute-start.1 = (bf16[384,512]{1,0:T(8,128)(2,1)S(1)}, bf16[384,512]{1,0:T(8,128)(2,1)S(1)}, u32[]{:S(2)}, u32[]{:S(2)}) collective-permute-start(bf16[384,512]{1,0:T(8,128)(2,1)S(1)} %get-tuple-element.276), channel_id=1, source_target_pairs={{1,0},{2,1},{3,2},{4,3},{5,4},{6,5},{7,6},{8,7},{9,8},{10,9},{11,1... | collective-permute-start | bytes 1179656 | tf_op jit(solution)/shard_map/while/body/eval_jaxpr/ppermute | solution.py:13
  99.1 32.6 %all-to-all-start.1 = ((f32[16,58,1]{1,2,0:T(1,128)}), f32[16,58,1]{1,2,0:T(1,128)S(1)}, u32[]{:S(2)}, u32[]{:S(2)}) async-start(f32[16,58,1]{1,2,0:T(1,128)} %bitcast.9), calls=%async_computation.1 | async-start | bytes 16384 | tf_op jit(solution)/shard_map/all_to_all | solution.py:121
Sparse Core Ops, SparseCore 0:
  33.7 96.6 all-reduce.1
where the time goes:
time: 143 us; the launch traced here: 142 us
  waiting for transfers between devices  60.5 us (42%)
  starting transfers between devices  34.8 us (24%)
  local copies, waits for them, and re-layouts  19.8 us (14%)
  between operations  14.3 us (10%)
  other arithmetic  7.29 us (5%)
  matrix products  5.41 us (4%)
    all_to_all x1, waiting for transfers between devices, sorted_density(): lax.all_to_all(packed, 'blk', split_axis=0, concat_axis=0, tiled=True)  22.5 us
    psum x1, waiting for transfers between devices, on_device(): centroid = lax.psum(partial_sum, 'blk')  22.5 us
    ppermute x6, starting transfers between devices, shifted(): return lax.ppermute(array, axis, pairs)  19.7 us
    ppermute x6, waiting for transfers between devices, shifted(): return lax.ppermute(array, axis, pairs)  15.5 us
    all_to_all x1, starting transfers between devices, sorted_density(): lax.all_to_all(returned, 'blk', split_axis=0, concat_axis=0, tiled=True)  8.78 us
    all_to_all x1, starting transfers between devices, sorted_density(): lax.all_to_all(packed, 'blk', split_axis=0, concat_axis=0, tiled=True)  6.3 us
    gather x2, local copies, waits for them, and re-layouts, sorted_density(): unit[sender]  4.29 us
    scatter x1, local copies, waits for them, and re-layouts, sorted_density(): sender = jnp.zeros((devices * capacity,), jnp.int32).at[address].set(jnp....  2.92 us
  transfers between devices with their start and end apart: 9, of which 5 were waited for; matrix products, arithmetic and copies ran while one was open for 8% of the time, Pallas kernels for 0%

commit v1 on v0

--- a/solution.py
+++ b/solution.py
@@ -5,6 +5,29 @@
 
 SOFTMAX_TEMP = 0.1
 EPSILON = 1e-06
+
+
+def cut_along(x, dim, devices):
+    lengths = x.shape
+    blocks = x.reshape(*lengths[:dim], devices, lengths[dim] // devices, *lengths[dim + 1 :])
+    return jnp.moveaxis(blocks, dim, 0)
+
+
+def joined_along(blocks, dim):
+    blocks = jnp.moveaxis(blocks, 0, dim)
+    dims = blocks.shape
+    return blocks.reshape(*dims[:dim], dims[dim] * dims[dim + 1], *dims[dim + 2 :])
+
+
+def rotated_exchange(x, axis, split_dim, concat_dim):
+    peers, position = (lax.axis_size(axis), lax.axis_index(axis))
+    pieces = cut_along(x, split_dim, peers)
+    outs = [pieces[position]]
+    for step in range(1, peers):
+        sent = pieces[(position + step) % peers]
+        outs.append(lax.ppermute(sent, axis, [(i, (i + step) % peers) for i in range(peers)]))
+    pieces = jnp.stack(outs)[(position - jnp.arange(peers)) % peers]
+    return joined_along(pieces, concat_dim)
 
 
 def shifted(array, axis, by):
@@ -71,7 +94,7 @@
     )
     filled = jnp.zeros((devices * capacity,), jnp.bool_).at[address].set(True)
     packed = jnp.where(filled[:, None], unit[sender], jnp.zeros((), jnp.bfloat16))
-    arrived = lax.all_to_all(packed, "blk", split_axis=0, concat_axis=0, tiled=True)
+    arrived = rotated_exchange(packed, "blk", 0, 0)
     local = jnp.arange(rows_dev, dtype=jnp.int32)
     places = own_index * rows_dev + local
     home_label = jnp.sum((places[:, None] >= ends[None, :]).astype(jnp.int32), axis=1)

time: 143 us -> 127 us (0.89)
  the two profiles are of different devices: /device:TPU:8 before, /device:TPU:0 now
where the time goes in v1:
time: 127 us; the launch traced here: 126 us
  starting transfers between devices  55.5 us (44%)
  waiting for transfers between devices  23.6 us (19%)
  local copies, waits for them, and re-layouts  20.6 us (16%)
  between operations  14.7 us (12%)
  other arithmetic  6.31 us (5%)
  matrix products  5.41 us (4%)
    ppermute x6, starting transfers between devices, shifted(): return lax.ppermute(array, axis, pairs)  23.7 us
    ppermute x15, starting transfers between devices, rotated_exchange(): lax.ppermute(sent, axis, [(i, (i + step) % peers) for i in range(peers)])  22.2 us
    all_to_all x1, starting transfers between devices, sorted_density(): lax.all_to_all(returned, 'blk', split_axis=0, concat_axis=0, tiled=True)  9.63 us
    ppermute x15, waiting for transfers between devices, rotated_exchange(): lax.ppermute(sent, axis, [(i, (i + step) % peers) for i in range(peers)])  9.49 us
    ppermute x6, waiting for transfers between devices, shifted(): return lax.ppermute(array, axis, pairs)  9.08 us
    all_to_all x1, waiting for transfers between devices, sorted_density(): lax.all_to_all(returned, 'blk', split_axis=0, concat_axis=0, tiled=True)  5.02 us
    gather x2, local copies, waits for them, and re-layouts, sorted_density(): unit[sender]  4.29 us
    scatter x1, local copies, waits for them, and re-layouts, sorted_density(): sender = jnp.zeros((devices * capacity,), jnp.int32).at[address].set(jnp....  2.92 us
  transfers between devices with their start and end apart: 23, of which 9 were waited for; matrix products, arithmetic and copies ran while one was open for 19% of the time, Pallas kernels for 0%

profile of v1, /device:TPU:0, one launch (start us, length us, event | category | flops | bytes accessed | tf_op | source)
XLA Modules:
  0.0 126.4 jit_solution(6832929182432511807)
XLA Ops:
  7.2 1.2 fusion.14
  8.6 0.5 copy-done.1
  9.1 0.8 fusion.18
  10.0 0.6 copy-done.2
  11.4 0.9 reduce-window.41
  12.3 0.2 slice_reduce_fusion
  12.6 0.2 select_reduce_fusion
  13.0 0.9 reduce-window.39
  13.9 0.2 slice_reduce_fusion.1
  14.2 0.3 convert_reduce_fusion.4
  14.5 0.3 convert_reduce_fusion.2
  14.8 2.9 %scatter_custom_fusion.1 = s32[928]{0:T(1024)S(1)} fusion(s32[384]{0:T(512)S(1)} %fusion.59, s32[384]{0:T(512)S(1)} %iota.61, s32[]{:T(128)} %copy.55), kind=kCustom, calls=%fused_computation.157 | custom fusion | bytes 3716 | tf_op jit(solution)/shard_map/scatter | solution.py:93
  17.9 4.0 %gather_fusion = bf16[928,512]{1,0:T(8,128)(2,1)S(1)} fusion(bf16[384,512]{1,0:T(8,128)(2,1)S(1)} %fusion.15, s32[1024]{0:T(1024)S(1)} %get-tuple-element.222), kind=kCustom, calls=%fused_computation | custom fusion | bytes 1904256 | tf_op jit(solution)/shard_map/gather | solution.py:96
  21.9 0.2 gather.15
  22.2 2.0 %scatter_custom_fusion = pred[928]{0:T(1024)(128)(4,1)S(1)} fusion(s32[384]{0:T(512)S(1)} %fusion.59, pred[384]{0:T(512)(128)(4,1)S(1)} %broadcast.549, pred[]{:T(512)} %constant.238.clone.1), kind=kCustom, calls=%fused_computation.170 | custom fusion | bytes 929 | tf_op jit(solution)/shard_map/scatter | solution.py:95
  24.3 0.2 broadcast_select_fusion
  24.8 0.5 collective-permute-start.2
  25.3 2.6 %collective-permute-start.3 = (bf16[58,512]{1,0:T(8,128)(2,1)S(1)}, bf16[58,512]{1,0:T(8,128)(2,1)S(1)}, u32[]{:S(2)}, u32[]{:S(2)}) collective-permute-start(bf16[58,512]{1,0:T(8,128)(2,1)S(1)} %get-tuple-element.207), channel_id=1, source_target_pairs={{0,2},{1,3},{2,4},{3,5},{4,6},{5,7},{6,8},{7,9},{8,10},{9,11},{10,... | collective-permute-start | bytes 178184 | tf_op jit(solution)/shard_map/ppermute | solution.py:28
  27.9 2.4 %collective-permute-start.4 = (bf16[58,512]{1,0:T(8,128)(2,1)S(1)}, bf16[58,512]{1,0:T(8,128)(2,1)S(1)}, u32[]{:S(2)}, u32[]{:S(2)}) collective-permute-start(bf16[58,512]{1,0:T(8,128)(2,1)S(1)} %get-tuple-element.206), channel_id=1, source_target_pairs={{0,3},{1,4},{2,5},{3,6},{4,7},{5,8},{6,9},{7,10},{8,11},{9,12},{10... | collective-permute-start | bytes 178184 | tf_op jit(solution)/shard_map/ppermute | solution.py:28
  30.3 1.6 %collective-permute-start.5 = (bf16[58,512]{1,0:T(8,128)(2,1)S(1)}, bf16[58,512]{1,0:T(8,128)(2,1)S(1)}, u32[]{:S(2)}, u32[]{:S(2)}) collective-permute-start(bf16[58,512]{1,0:T(8,128)(2,1)S(1)} %get-tuple-element.205), channel_id=1, source_target_pairs={{0,4},{1,5},{2,6},{3,7},{4,8},{5,9},{6,10},{7,11},{8,12},{9,13},{1... | collective-permute-start | bytes 178184 | tf_op jit(solution)/shard_map/ppermute | solution.py:28
  31.9 0.2 collective-permute-start.6
  32.1 0.2 collective-permute-done.2
  32.3 1.0 collective-permute-start.7
  33.4 4.4 %collective-permute-start.8 = (bf16[58,512]{1,0:T(8,128)(2,1)S(1)}, bf16[58,512]{1,0:T(8,128)(2,1)S(1)}, u32[]{:S(2)}, u32[]{:S(2)}) collective-permute-start(bf16[58,512]{1,0:T(8,128)(2,1)S(1)} %get-tuple-element.202), channel_id=1, source_target_pairs={{0,7},{1,8},{2,9},{3,10},{4,11},{5,12},{6,13},{7,14},{8,15},{9,0},... | collective-permute-start | bytes 178184 | tf_op jit(solution)/shard_map/ppermute | solution.py:28
  37.8 0.4 collective-permute-start.9
  38.2 0.3 collective-permute-start.10
  38.5 6.6 %collective-permute-done.6 = bf16[58,512]{1,0:T(8,128)(2,1)S(1)} collective-permute-done((bf16[58,512]{1,0:T(8,128)(2,1)S(1)}, bf16[58,512]{1,0:T(8,128)(2,1)S(1)}, u32[]{:S(2)}, u32[]{:S(2)}) %collective-permute-start.6) | collective-permute-done | bytes 59424 | tf_op jit(solution)/shard_map/ppermute | solution.py:28
  45.2 0.2 collective-permute-done.7
  45.4 0.5 collective-permute-start.12
  45.9 3.9 %collective-permute-start.13 = (bf16[58,512]{1,0:T(8,128)(2,1)S(1)}, bf16[58,512]{1,0:T(8,128)(2,1)S(1)}, u32[]{:S(2)}, u32[]{:S(2)}) collective-permute-start(bf16[58,512]{1,0:T(8,128)(2,1)S(1)} %get-tuple-element.197), channel_id=1, source_target_pairs={{0,12},{1,13},{2,14},{3,15},{4,0},{5,1},{6,2},{7,3},{8,4},{9,5},{1... | collective-permute-start | bytes 178184 | tf_op jit(solution)/shard_map/ppermute | solution.py:28
  49.8 0.8 collective-permute-start.14
  50.6 2.7 %collective-permute-start.15 = (bf16[58,512]{1,0:T(8,128)(2,1)S(1)}, bf16[58,512]{1,0:T(8,128)(2,1)S(1)}, u32[]{:S(2)}, u32[]{:S(2)}) collective-permute-start(bf16[58,512]{1,0:T(8,128)(2,1)S(1)} %get-tuple-element.195), channel_id=1, source_target_pairs={{0,14},{1,15},{2,0},{3,1},{4,2},{5,3},{6,4},{7,5},{8,6},{9,7},{10,... | collective-permute-start | bytes 178184 | tf_op jit(solution)/shard_map/ppermute | solution.py:28
  53.3 0.9 collective-permute-start.16
  54.2 1.5 %collective-permute-done.15 = bf16[58,512]{1,0:T(8,128)(2,1)S(1)} collective-permute-done((bf16[58,512]{1,0:T(8,128)(2,1)S(1)}, bf16[58,512]{1,0:T(8,128)(2,1)S(1)}, u32[]{:S(2)}, u32[]{:S(2)}) %collective-permute-start.15) | collective-permute-done | bytes 59424 | tf_op jit(solution)/shard_map/ppermute | solution.py:28
  55.8 0.9 collective-permute-done.16
  56.6 0.6 gather_fusion.1
  57.3 0.3 reshape.459
  57.5 2.1 %gather_fusion.2 = bf16[384,512]{1,0:T(8,128)(2,1)S(1)} fusion(bf16[928,512]{1,0:T(8,128)(2,1)S(1)} %reshape.459, s32[1024]{0:T(1024)S(1)} %get-tuple-element.221), kind=kCustom, calls=%fused_computation.2 | custom fusion | bytes 787968 | tf_op jit(solution)/shard_map/gather | solution.py:118
  59.7 0.4 fusion.12
  60.1 36.0 %while.18 = (s32[]{:T(128)}, bf16[384,512]{1,0:T(8,128)(2,1)S(1)}, bf16[384,512]{1,0:T(8,128)(2,1)S(1)}, f32[384]{0:T(512)S(1)}, s32[384]{0:T(512)S(1)}, /*index...) while((s32[]{:T(128)}, bf16[384,512]{1,0:T(8,128)(2,1)S(1)}, ...), condition=%wide.region_26.27_spmd.clone, body=%wide.region_21.26_spmd.clone.sunk | while | flops 303321984 | bytes 6322649 | solution.py:139
  60.1 3.4 %collective-permute-start = (bf16[384,512]{1,0:T(8,128)(2,1)S(1)}, bf16[384,512]{1,0:T(8,128)(2,1)S(1)}, u32[]{:S(2)}, u32[]{:S(2)}) collective-permute-start(bf16[384,512]{1,0:T(8,128)(2,1)S(1)} %get-tuple-element.291), channel_id=1, source_target_pairs={{0,1},{1,2},{2,3},{3,4},{4,5},{5,6},{6,7},{7,8},{8,9},{9,10},{10,1... | collective-permute-start | bytes 1179656 | tf_op jit(solution)/shard_map/while/body/eval_jaxpr/ppermute | solution.py:36
  63.5 1.3 %collective-permute-start.1 = (bf16[384,512]{1,0:T(8,128)(2,1)S(1)}, bf16[384,512]{1,0:T(8,128)(2,1)S(1)}, u32[]{:S(2)}, u32[]{:S(2)}) collective-permute-start(bf16[384,512]{1,0:T(8,128)(2,1)S(1)} %get-tuple-element.292), channel_id=1, source_target_pairs={{1,0},{2,1},{3,2},{4,3},{5,4},{6,5},{7,6},{8,7},{9,8},{10,9},{11,1... | collective-permute-start | bytes 1179656 | tf_op jit(solution)/shard_map/while/body/eval_jaxpr/ppermute | solution.py:36
  65.0 2.4 %collective-permute-done.1 = bf16[384,512]{1,0:T(8,128)(2,1)S(1)} collective-permute-done((bf16[384,512]{1,0:T(8,128)(2,1)S(1)}, bf16[384,512]{1,0:T(8,128)(2,1)S(1)}, u32[]{:S(2)}, u32[]{:S(2)}) %collective-permute-start.1) | collective-permute-done | bytes 393248 | tf_op jit(solution)/shard_map/while/body/eval_jaxpr/ppermute | solution.py:36
  67.4 0.4 fusion.91
  67.8 0.4 fusion.92
  68.3 8.5 %collective-permute-start = (bf16[384,512]{1,0:T(8,128)(2,1)S(1)}, bf16[384,512]{1,0:T(8,128)(2,1)S(1)}, u32[]{:S(2)}, u32[]{:S(2)}) collective-permute-start(bf16[384,512]{1,0:T(8,128)(2,1)S(1)} %get-tuple-element.291), channel_id=1, source_target_pairs={{0,1},{1,2},{2,3},{3,4},{4,5},{5,6},{6,7},{7,8},{8,9},{9,10},{10,1... | collective-permute-start | bytes 1179656 | tf_op jit(solution)/shard_map/while/body/eval_jaxpr/ppermute | solution.py:36
  76.8 1.3 %collective-permute-start.1 = (bf16[384,512]{1,0:T(8,128)(2,1)S(1)}, bf16[384,512]{1,0:T(8,128)(2,1)S(1)}, u32[]{:S(2)}, u32[]{:S(2)}) collective-permute-start(bf16[384,512]{1,0:T(8,128)(2,1)S(1)} %get-tuple-element.292), channel_id=1, source_target_pairs={{1,0},{2,1},{3,2},{4,3},{5,4},{6,5},{7,6},{8,7},{9,8},{10,9},{11,1... | collective-permute-start | bytes 1179656 | tf_op jit(solution)/shard_map/while/body/eval_jaxpr/ppermute | solution.py:36
  78.2 3.1 %collective-permute-done.1 = bf16[384,512]{1,0:T(8,128)(2,1)S(1)} collective-permute-done((bf16[384,512]{1,0:T(8,128)(2,1)S(1)}, bf16[384,512]{1,0:T(8,128)(2,1)S(1)}, u32[]{:S(2)}, u32[]{:S(2)}) %collective-permute-start.1) | collective-permute-done | bytes 393248 | tf_op jit(solution)/shard_map/while/body/eval_jaxpr/ppermute | solution.py:36
  81.4 0.4 fusion.91
  81.8 0.4 fusion.92
  82.3 7.9 %collective-permute-start = (bf16[384,512]{1,0:T(8,128)(2,1)S(1)}, bf16[384,512]{1,0:T(8,128)(2,1)S(1)}, u32[]{:S(2)}, u32[]{:S(2)}) collective-permute-start(bf16[384,512]{1,0:T(8,128)(2,1)S(1)} %get-tuple-element.291), channel_id=1, source_target_pairs={{0,1},{1,2},{2,3},{3,4},{4,5},{5,6},{6,7},{7,8},{8,9},{9,10},{10,1... | collective-permute-start | bytes 1179656 | tf_op jit(solution)/shard_map/while/body/eval_jaxpr/ppermute | solution.py:36
  90.2 1.3 %collective-permute-start.1 = (bf16[384,512]{1,0:T(8,128)(2,1)S(1)}, bf16[384,512]{1,0:T(8,128)(2,1)S(1)}, u32[]{:S(2)}, u32[]{:S(2)}) collective-permute-start(bf16[384,512]{1,0:T(8,128)(2,1)S(1)} %get-tuple-element.292), channel_id=1, source_target_pairs={{1,0},{2,1},{3,2},{4,3},{5,4},{6,5},{7,6},{8,7},{9,8},{10,9},{11,1... | collective-permute-start | bytes 1179656 | tf_op jit(solution)/shard_map/while/body/eval_jaxpr/ppermute | solution.py:36
  91.6 3.5 %collective-permute-done.1 = bf16[384,512]{1,0:T(8,128)(2,1)S(1)} collective-permute-done((bf16[384,512]{1,0:T(8,128)(2,1)S(1)}, bf16[384,512]{1,0:T(8,128)(2,1)S(1)}, u32[]{:S(2)}, u32[]{:S(2)}) %collective-permute-start.1) | collective-permute-done | bytes 393248 | tf_op jit(solution)/shard_map/while/body/eval_jaxpr/ppermute | solution.py:36
  95.2 0.4 fusion.91
  95.6 0.4 fusion.92
  96.1 2.9 %scatter_custom_fusion.2 = f32[928]{0:T(1024)S(1)} fusion(s32[384]{0:T(512)S(1)} %fusion.58, f32[384]{0:T(512)S(1)} %get-tuple-element.141, f32[]{:T(128)} %constant.225.clone.1), kind=kCustom, calls=%fused_computation.165 | custom fusion | bytes 3716 | tf_op jit(solution)/shard_map/scatter | solution.py:142
  99.0 0.7 all_to_all.8
  99.7 9.6 %all-to-all-start = ((f32[16,58,1]{1,2,0:T(1,128)}), f32[16,58,1]{1,2,0:T(1,128)S(1)}, u32[]{:S(2)}, u32[]{:S(2)}) async-start(f32[16,58,1]{1,2,0:T(1,128)} %bitcast.40), calls=%async_computation | async-start | bytes 16384 | tf_op jit(solution)/shard_map/all_to_all | solution.py:144
  109.4 1.4 %fusion.13 = f32[384]{0:T(512)S(1)} fusion(bf16[384,512]{1,0:T(8,128)(2,1)S(1)} %fusion.15, f32[64,512]{1,0:T(8,128)} %all-reduce.2.cloned.1.call-done, s32[384]{0:T(512)S(1)} %copy-done.1), kind=kOutput, calls=%fused_computation.29 | convolution fusion | flops 151068288 | bytes 527360 | tf_op jit(solution)/shard_map/dot_general | solution.py:159
  110.8 5.0 %all-to-all-done = f32[16,58,1]{1,2,0:T(1,128)S(1)} async-done(((f32[16,58,1]{1,2,0:T(1,128)}), f32[16,58,1]{1,2,0:T(1,128)S(1)}, u32[]{:S(2)}, u32[]{:S(2)}) %all-to-all-start) | async-done | bytes 3744 | tf_op jit(solution)/shard_map/all_to_all | solution.py:144
  115.8 0.5 broadcast.633
  116.3 0.7 reduce.13
  117.1 1.9 %gather_fusion.3 = f32[384]{0:T(512)S(1)} fusion(f32[928]{0:T(1024)S(1)} %all_to_all.10, s32[1024]{0:T(1024)S(1)} %pad_clamp_fusion), kind=kCustom, calls=%fused_computation.3 | custom fusion | bytes 4608 | tf_op jit(solution)/shard_map/gather | solution.py:145
  119.0 0.6 convert_divide_fusion
  (93 shorter events, 2.4 us)
Async XLA Ops:
  7.2 1.3 copy-start
  7.2 102.2 %all-reduce.2.cloned.1.call-start = ((), (), s32[]{:S(2)}) async-start(), calls=%async_computation.1 | async-start | bytes 262144 | tf_op jit(solution)/shard_map/psum | solution.py:155
  8.4 0.7 copy-start.1
  10.0 0.7 copy-start.2
  24.8 7.6 %collective-permute-start.2 = (bf16[58,512]{1,0:T(8,128)(2,1)S(1)}, bf16[58,512]{1,0:T(8,128)(2,1)S(1)}, u32[]{:S(2)}, u32[]{:S(2)}) collective-permute-start(bf16[58,512]{1,0:T(8,128)(2,1)S(1)} %get-tuple-element.208), channel_id=1, source_target_pairs={{0,1},{1,2},{2,3},{3,4},{4,5},{5,6},{6,7},{7,8},{8,9},{9,10},{10,1... | collective-permute-start | bytes 178184 | tf_op jit(solution)/shard_map/ppermute | solution.py:28
  25.3 8.1 %collective-permute-start.3 = (bf16[58,512]{1,0:T(8,128)(2,1)S(1)}, bf16[58,512]{1,0:T(8,128)(2,1)S(1)}, u32[]{:S(2)}, u32[]{:S(2)}) collective-permute-start(bf16[58,512]{1,0:T(8,128)(2,1)S(1)} %get-tuple-element.207), channel_id=1, source_target_pairs={{0,2},{1,3},{2,4},{3,5},{4,6},{5,7},{6,8},{7,9},{8,10},{9,11},{10,... | collective-permute-start | bytes 178184 | tf_op jit(solution)/shard_map/ppermute | solution.py:28
  27.9 9.9 %collective-permute-start.4 = (bf16[58,512]{1,0:T(8,128)(2,1)S(1)}, bf16[58,512]{1,0:T(8,128)(2,1)S(1)}, u32[]{:S(2)}, u32[]{:S(2)}) collective-permute-start(bf16[58,512]{1,0:T(8,128)(2,1)S(1)} %get-tuple-element.206), channel_id=1, source_target_pairs={{0,3},{1,4},{2,5},{3,6},{4,7},{5,8},{6,9},{7,10},{8,11},{9,12},{10... | collective-permute-start | bytes 178184 | tf_op jit(solution)/shard_map/ppermute | solution.py:28
  30.3 7.9 %collective-permute-start.5 = (bf16[58,512]{1,0:T(8,128)(2,1)S(1)}, bf16[58,512]{1,0:T(8,128)(2,1)S(1)}, u32[]{:S(2)}, u32[]{:S(2)}) collective-permute-start(bf16[58,512]{1,0:T(8,128)(2,1)S(1)} %get-tuple-element.205), channel_id=1, source_target_pairs={{0,4},{1,5},{2,6},{3,7},{4,8},{5,9},{6,10},{7,11},{8,12},{9,13},{1... | collective-permute-start | bytes 178184 | tf_op jit(solution)/shard_map/ppermute | solution.py:28
  31.9 13.3 %collective-permute-start.6 = (bf16[58,512]{1,0:T(8,128)(2,1)S(1)}, bf16[58,512]{1,0:T(8,128)(2,1)S(1)}, u32[]{:S(2)}, u32[]{:S(2)}) collective-permute-start(bf16[58,512]{1,0:T(8,128)(2,1)S(1)} %get-tuple-element.204), channel_id=1, source_target_pairs={{0,5},{1,6},{2,7},{3,8},{4,9},{5,10},{6,11},{7,12},{8,13},{9,14},{... | collective-permute-start | bytes 178184 | tf_op jit(solution)/shard_map/ppermute | solution.py:28
  32.3 13.1 %collective-permute-start.7 = (bf16[58,512]{1,0:T(8,128)(2,1)S(1)}, bf16[58,512]{1,0:T(8,128)(2,1)S(1)}, u32[]{:S(2)}, u32[]{:S(2)}) collective-permute-start(bf16[58,512]{1,0:T(8,128)(2,1)S(1)} %get-tuple-element.203), channel_id=1, source_target_pairs={{0,6},{1,7},{2,8},{3,9},{4,10},{5,11},{6,12},{7,13},{8,14},{9,15},... | collective-permute-start | bytes 178184 | tf_op jit(solution)/shard_map/ppermute | solution.py:28
  33.4 12.5 %collective-permute-start.8 = (bf16[58,512]{1,0:T(8,128)(2,1)S(1)}, bf16[58,512]{1,0:T(8,128)(2,1)S(1)}, u32[]{:S(2)}, u32[]{:S(2)}) collective-permute-start(bf16[58,512]{1,0:T(8,128)(2,1)S(1)} %get-tuple-element.202), channel_id=1, source_target_pairs={{0,7},{1,8},{2,9},{3,10},{4,11},{5,12},{6,13},{7,14},{8,15},{9,0},... | collective-permute-start | bytes 178184 | tf_op jit(solution)/shard_map/ppermute | solution.py:28
  37.8 12.0 %collective-permute-start.9 = (bf16[58,512]{1,0:T(8,128)(2,1)S(1)}, bf16[58,512]{1,0:T(8,128)(2,1)S(1)}, u32[]{:S(2)}, u32[]{:S(2)}) collective-permute-start(bf16[58,512]{1,0:T(8,128)(2,1)S(1)} %get-tuple-element.201), channel_id=1, source_target_pairs={{0,8},{1,9},{2,10},{3,11},{4,12},{5,13},{6,14},{7,15},{8,0},{9,1},... | collective-permute-start | bytes 178184 | tf_op jit(solution)/shard_map/ppermute | solution.py:28
  38.2 12.4 %collective-permute-start.10 = (bf16[58,512]{1,0:T(8,128)(2,1)S(1)}, bf16[58,512]{1,0:T(8,128)(2,1)S(1)}, u32[]{:S(2)}, u32[]{:S(2)}) collective-permute-start(bf16[58,512]{1,0:T(8,128)(2,1)S(1)} %get-tuple-element.200), channel_id=1, source_target_pairs={{0,9},{1,10},{2,11},{3,12},{4,13},{5,14},{6,15},{7,0},{8,1},{9,2},... | collective-permute-start | bytes 178184 | tf_op jit(solution)/shard_map/ppermute | solution.py:28
  45.2 8.1 %collective-permute-start.11 = (bf16[58,512]{1,0:T(8,128)(2,1)S(1)}, bf16[58,512]{1,0:T(8,128)(2,1)S(1)}, u32[]{:S(2)}, u32[]{:S(2)}) collective-permute-start(bf16[58,512]{1,0:T(8,128)(2,1)S(1)} %get-tuple-element.199), channel_id=1, source_target_pairs={{0,10},{1,11},{2,12},{3,13},{4,14},{5,15},{6,0},{7,1},{8,2},{9,3},... | collective-permute-start | bytes 178184 | tf_op jit(solution)/shard_map/ppermute | solution.py:28
  45.4 8.8 %collective-permute-start.12 = (bf16[58,512]{1,0:T(8,128)(2,1)S(1)}, bf16[58,512]{1,0:T(8,128)(2,1)S(1)}, u32[]{:S(2)}, u32[]{:S(2)}) collective-permute-start(bf16[58,512]{1,0:T(8,128)(2,1)S(1)} %get-tuple-element.198), channel_id=1, source_target_pairs={{0,11},{1,12},{2,13},{3,14},{4,15},{5,0},{6,1},{7,2},{8,3},{9,4},{... | collective-permute-start | bytes 178184 | tf_op jit(solution)/shard_map/ppermute | solution.py:28
  45.9 8.3 %collective-permute-start.13 = (bf16[58,512]{1,0:T(8,128)(2,1)S(1)}, bf16[58,512]{1,0:T(8,128)(2,1)S(1)}, u32[]{:S(2)}, u32[]{:S(2)}) collective-permute-start(bf16[58,512]{1,0:T(8,128)(2,1)S(1)} %get-tuple-element.197), channel_id=1, source_target_pairs={{0,12},{1,13},{2,14},{3,15},{4,0},{5,1},{6,2},{7,3},{8,4},{9,5},{1... | collective-permute-start | bytes 178184 | tf_op jit(solution)/shard_map/ppermute | solution.py:28
  49.8 4.4 %collective-permute-start.14 = (bf16[58,512]{1,0:T(8,128)(2,1)S(1)}, bf16[58,512]{1,0:T(8,128)(2,1)S(1)}, u32[]{:S(2)}, u32[]{:S(2)}) collective-permute-start(bf16[58,512]{1,0:T(8,128)(2,1)S(1)} %get-tuple-element.196), channel_id=1, source_target_pairs={{0,13},{1,14},{2,15},{3,0},{4,1},{5,2},{6,3},{7,4},{8,5},{9,6},{10... | collective-permute-start | bytes 178184 | tf_op jit(solution)/shard_map/ppermute | solution.py:28
  50.6 5.2 %collective-permute-start.15 = (bf16[58,512]{1,0:T(8,128)(2,1)S(1)}, bf16[58,512]{1,0:T(8,128)(2,1)S(1)}, u32[]{:S(2)}, u32[]{:S(2)}) collective-permute-start(bf16[58,512]{1,0:T(8,128)(2,1)S(1)} %get-tuple-element.195), channel_id=1, source_target_pairs={{0,14},{1,15},{2,0},{3,1},{4,2},{5,3},{6,4},{7,5},{8,6},{9,7},{10,... | collective-permute-start | bytes 178184 | tf_op jit(solution)/shard_map/ppermute | solution.py:28
  53.3 3.4 %collective-permute-start.16 = (bf16[58,512]{1,0:T(8,128)(2,1)S(1)}, bf16[58,512]{1,0:T(8,128)(2,1)S(1)}, u32[]{:S(2)}, u32[]{:S(2)}) collective-permute-start(bf16[58,512]{1,0:T(8,128)(2,1)S(1)} %get-tuple-element.194), channel_id=1, source_target_pairs={{0,15},{1,0},{2,1},{3,2},{4,3},{5,4},{6,5},{7,6},{8,7},{9,8},{10,9... | collective-permute-start | bytes 178184 | tf_op jit(solution)/shard_map/ppermute | solution.py:28
  60.1 7.7 %collective-permute-start = (bf16[384,512]{1,0:T(8,128)(2,1)S(1)}, bf16[384,512]{1,0:T(8,128)(2,1)S(1)}, u32[]{:S(2)}, u32[]{:S(2)}) collective-permute-start(bf16[384,512]{1,0:T(8,128)(2,1)S(1)} %get-tuple-element.291), channel_id=1, source_target_pairs={{0,1},{1,2},{2,3},{3,4},{4,5},{5,6},{6,7},{7,8},{8,9},{9,10},{10,1... | collective-permute-start | bytes 1179656 | tf_op jit(solution)/shard_map/while/body/eval_jaxpr/ppermute | solution.py:36
  63.5 3.9 %collective-permute-start.1 = (bf16[384,512]{1,0:T(8,128)(2,1)S(1)}, bf16[384,512]{1,0:T(8,128)(2,1)S(1)}, u32[]{:S(2)}, u32[]{:S(2)}) collective-permute-start(bf16[384,512]{1,0:T(8,128)(2,1)S(1)} %get-tuple-element.292), channel_id=1, source_target_pairs={{1,0},{2,1},{3,2},{4,3},{5,4},{6,5},{7,6},{8,7},{9,8},{10,9},{11,1... | collective-permute-start | bytes 1179656 | tf_op jit(solution)/shard_map/while/body/eval_jaxpr/ppermute | solution.py:36
  68.3 13.5 %collective-permute-start = (bf16[384,512]{1,0:T(8,128)(2,1)S(1)}, bf16[384,512]{1,0:T(8,128)(2,1)S(1)}, u32[]{:S(2)}, u32[]{:S(2)}) collective-permute-start(bf16[384,512]{1,0:T(8,128)(2,1)S(1)} %get-tuple-element.291), channel_id=1, source_target_pairs={{0,1},{1,2},{2,3},{3,4},{4,5},{5,6},{6,7},{7,8},{8,9},{9,10},{10,1... | collective-permute-start | bytes 1179656 | tf_op jit(solution)/shard_map/while/body/eval_jaxpr/ppermute | solution.py:36
  76.8 4.6 %collective-permute-start.1 = (bf16[384,512]{1,0:T(8,128)(2,1)S(1)}, bf16[384,512]{1,0:T(8,128)(2,1)S(1)}, u32[]{:S(2)}, u32[]{:S(2)}) collective-permute-start(bf16[384,512]{1,0:T(8,128)(2,1)S(1)} %get-tuple-element.292), channel_id=1, source_target_pairs={{1,0},{2,1},{3,2},{4,3},{5,4},{6,5},{7,6},{8,7},{9,8},{10,9},{11,1... | collective-permute-start | bytes 1179656 | tf_op jit(solution)/shard_map/while/body/eval_jaxpr/ppermute | solution.py:36
  82.3 13.3 %collective-permute-start = (bf16[384,512]{1,0:T(8,128)(2,1)S(1)}, bf16[384,512]{1,0:T(8,128)(2,1)S(1)}, u32[]{:S(2)}, u32[]{:S(2)}) collective-permute-start(bf16[384,512]{1,0:T(8,128)(2,1)S(1)} %get-tuple-element.291), channel_id=1, source_target_pairs={{0,1},{1,2},{2,3},{3,4},{4,5},{5,6},{6,7},{7,8},{8,9},{9,10},{10,1... | collective-permute-start | bytes 1179656 | tf_op jit(solution)/shard_map/while/body/eval_jaxpr/ppermute | solution.py:36
  90.2 5.0 %collective-permute-start.1 = (bf16[384,512]{1,0:T(8,128)(2,1)S(1)}, bf16[384,512]{1,0:T(8,128)(2,1)S(1)}, u32[]{:S(2)}, u32[]{:S(2)}) collective-permute-start(bf16[384,512]{1,0:T(8,128)(2,1)S(1)} %get-tuple-element.292), channel_id=1, source_target_pairs={{1,0},{2,1},{3,2},{4,3},{5,4},{6,5},{7,6},{8,7},{9,8},{10,9},{11,1... | collective-permute-start | bytes 1179656 | tf_op jit(solution)/shard_map/while/body/eval_jaxpr/ppermute | solution.py:36
  99.7 16.1 %all-to-all-start = ((f32[16,58,1]{1,2,0:T(1,128)}), f32[16,58,1]{1,2,0:T(1,128)S(1)}, u32[]{:S(2)}, u32[]{:S(2)}) async-start(f32[16,58,1]{1,2,0:T(1,128)} %bitcast.40), calls=%async_computation | async-start | bytes 16384 | tf_op jit(solution)/shard_map/all_to_all | solution.py:144
Sparse Core Ops, SparseCore 0:
  11.4 95.9 all-reduce.1
